TPU v7x, 32 devices: a whole 2x2x4 slice. The times are simulated.
32 devices in a mesh: prow: 8 (over z, x), pcol: 4 (over y, core).
Axes of the slice: x: 2, y: 2, z: 4, core: 2. Of those that a mesh axis runs over, the one named last changes fastest.
Arguments:
- matrix: float32 [16384, 16384], P('prow', 'pcol'), may hold values from -6 to 6
Outputs:
- reduced: float32 [16384, 16384], P('prow', 'pcol')
- householder_coefficients: float32 [2, 8], replicated
All inputs are finite; a program needn't handle non-finite values.
Results may differ from a plain program's by a relative error of at most 0.0003.
Values sent between devices are 32-bit elements; how exact they have to be, the bound alone decides.
A program may use at most 128 MiB of HBM per device.

v0:
```python
import jax
import jax.numpy as jnp
from jax import lax
from jax.sharding import PartitionSpec as P

NB = 8


epsilon = 1e-06


def from_root(x, axis, root):
    mine = lax.axis_index(axis) == root
    return lax.psum(jnp.where(mine, x, jnp.zeros_like(x)), axis)


def precise_dot(left, right):
    return jnp.dot(left, right, precision=lax.Precision.HIGHEST)


def inner_rows(left, right):
    return lax.dot_general(left, right, (((1,), (1,)), ((), ())), precision=lax.Precision.HIGHEST)


def householder(alpha_value, sumsq):
    norm_value = jnp.sqrt(sumsq + epsilon)
    signum = jnp.where(alpha_value >= 0.0, 1.0, -1.0).astype(jnp.float32)
    beta_value = -signum * norm_value
    return (beta_value, (beta_value - alpha_value) / beta_value, alpha_value - beta_value)


def per_device(matrix):
    rows_dev, cols_dev = matrix.shape
    prow_id = lax.axis_index("prow")
    pcol_id = lax.axis_index("pcol")
    row_glob = prow_id * rows_dev + jnp.arange(rows_dev, dtype=jnp.int32)
    col_glob = pcol_id * cols_dev + jnp.arange(cols_dev, dtype=jnp.int32)
    panel_index = jnp.arange(NB, dtype=jnp.int32)
    wide_index = jnp.arange(NB + 1, dtype=jnp.int32)
    held_tile = matrix
    source_side_factor_list = []
    target_side_factor_list = []
    column_owner_rank = 0 // cols_dev
    column_local_index = 0 - column_owner_rank * cols_dev
    row_root = 0 // rows_dev
    row_local = 0 - row_root * rows_dev
    col_panel = from_root(
        held_tile[:, column_local_index : column_local_index + NB + 1].T, "pcol", column_owner_rank
    )
    row_panel = from_root(held_tile[row_local : row_local + NB, :], "prow", row_root)
    sel_rows = (row_glob[None, :] == 0 + panel_index[:, None]).astype(jnp.float32)
    sel_cols = (col_glob[None, :] == 0 + wide_index[:, None]).astype(jnp.float32)
    v_rows = jnp.zeros((NB, rows_dev), jnp.float32)
    x_rows = jnp.zeros((NB, rows_dev), jnp.float32)
    y_cols = jnp.zeros((NB, cols_dev), jnp.float32)
    u_cols = jnp.zeros((NB, cols_dev), jnp.float32)
    v_panel = jnp.zeros((NB, NB), jnp.float32)
    y_panel = jnp.zeros((NB, NB + 1), jnp.float32)
    u_panel = jnp.zeros((NB, NB + 1), jnp.float32)
    diagonal_entries = []
    super_list = []
    for i in range(NB):
        column = (
            col_panel[i] - precise_dot(y_panel[:, i], v_rows) - precise_dot(u_panel[:, i], x_rows)
        )
        masked = jnp.where(row_glob >= i, column, 0.0)
        trans_part, v_coef, x_coef, col_window, col_sumsq, x_panel = lax.psum(
            (
                precise_dot(masked, held_tile),
                precise_dot(v_rows, masked),
                precise_dot(x_rows, masked),
                precise_dot(sel_rows, masked),
                jnp.sum(masked * masked),
                inner_rows(x_rows, sel_rows),
            ),
            "prow",
        )
        row_raw = row_panel[i]
        beta_left, source_side_coefficient, denom_left = householder(col_window[i], col_sumsq)
        row_eff = row_raw - precise_dot(v_panel[:, i], y_cols) - precise_dot(x_panel[:, i], u_cols)
        transposed = (
            trans_part
            - precise_dot(v_coef, y_cols)
            - precise_dot(x_coef, u_cols)
            - beta_left * row_eff
        ) / denom_left
        y_new = jnp.where(col_glob > i, source_side_coefficient * transposed, 0.0)
        v_new = (masked - beta_left * (row_glob == i).astype(jnp.float32)) / denom_left
        v_panel = v_panel.at[i].set(
            (col_window - beta_left * (panel_index == i).astype(jnp.float32)) / denom_left
        )
        v_rows = v_rows.at[i].set(v_new)
        y_cols = y_cols.at[i].set(y_new)
        row_new = row_eff - y_new
        row_masked = jnp.where(col_glob >= i + 1, row_new, 0.0)
        prod_part, y_coef, u_coef, row_window, row_sumsq, y_panel = lax.psum(
            (
                precise_dot(held_tile, row_masked),
                precise_dot(y_cols, row_masked),
                precise_dot(u_cols, row_masked),
                precise_dot(sel_cols, row_masked),
                jnp.sum(row_masked * row_masked),
                inner_rows(y_cols, sel_cols),
            ),
            "pcol",
        )
        right_reflector_beta, target_side_coefficient, denom_right = householder(
            row_window[i + 1], row_sumsq
        )
        column_next = (
            col_panel[i + 1]
            - precise_dot(y_panel[:, i + 1], v_rows)
            - precise_dot(u_panel[:, i + 1], x_rows)
        )
        product = (
            prod_part
            - precise_dot(y_coef, v_rows)
            - precise_dot(u_coef, x_rows)
            - right_reflector_beta * column_next
        ) / denom_right
        x_new = jnp.where(row_glob > i, target_side_coefficient * product, 0.0)
        u_new = (
            row_masked - right_reflector_beta * (col_glob == i + 1).astype(jnp.float32)
        ) / denom_right
        u_panel = u_panel.at[i].set(
            (row_window - right_reflector_beta * (wide_index == i + 1).astype(jnp.float32))
            / denom_right
        )
        x_rows = x_rows.at[i].set(x_new)
        u_cols = u_cols.at[i].set(u_new)
        diagonal_entries.append(beta_left)
        super_list.append(right_reflector_beta)
        source_side_factor_list.append(source_side_coefficient)
        target_side_factor_list.append(target_side_coefficient)
    stack_left = jnp.concatenate([v_rows, x_rows], axis=0)
    stack_right = jnp.concatenate([y_cols, u_cols], axis=0)
    updated = held_tile - lax.dot_general(
        stack_left, stack_right, (((0,), (0,)), ((), ())), precision=lax.Precision.HIGHEST
    )
    col_slice = updated[:, column_local_index : column_local_index + NB]
    col_keep = jnp.logical_and(pcol_id == column_owner_rank, row_glob >= NB)[:, None]
    updated = updated.at[:, column_local_index : column_local_index + NB].set(
        jnp.where(col_keep, v_rows.T, col_slice)
    )
    row_slice = updated[row_local : row_local + NB, :]
    panel_rows_glob = (0 + panel_index)[:, None]
    col_g = col_glob[None, :]
    v_window = jnp.where(panel_index[None, :] < panel_index[:, None], v_panel.T, 0.0)
    v_part = precise_dot(v_window, sel_cols[:NB])
    diag_arr = jnp.stack(diagonal_entries)[:, None]
    super_arr = jnp.stack(super_list)[:, None]
    panel_values = jnp.where(
        col_g < 0,
        row_slice,
        jnp.where(
            col_g < panel_rows_glob,
            v_part,
            jnp.where(
                col_g == panel_rows_glob,
                diag_arr,
                jnp.where(col_g == panel_rows_glob + 1, super_arr, u_cols),
            ),
        ),
    )
    row_final = jnp.where(prow_id == row_root, panel_values, row_slice)
    held_tile = updated.at[row_local : row_local + NB, :].set(row_final)
    householder_coefficients = jnp.stack(
        [jnp.stack(source_side_factor_list), jnp.stack(target_side_factor_list)]
    )
    return (held_tile, householder_coefficients)


def solution(mesh):
    in_specs = (P("prow", "pcol"),)
    out_specs = (P("prow", "pcol"), P())
    return jax.shard_map(
        per_device, mesh=mesh, in_specs=in_specs, out_specs=out_specs, check_vma=False
    )
```

profile of v0, /device:TPU:0, one launch (start us, length us, event | category | flops | bytes accessed | tf_op | source)
XLA Modules:
  0.0 1049.0 jit_solution(7705097731152169826)
XLA Ops:
  7.2 2.3 select_bitcast_fusion
  9.6 1.6 slice_select_fusion
  14.8 35.1 %all-reduce.25.cloned.1.call-done = f32[9,2048]{0,1:T(8,128)} async-done(((f32[9,2048]{0,1:T(8,128)}), f32[9,2048]{0,1:T(8,128)}) %all-reduce.25.cloned.1.call-update) | async-done | bytes 73744 | tf_op jit(solution)/shard_map/psum | solution.py:14
  49.9 10.3 slice_reduce_fusion
  60.9 19.6 %fusion.321 = f32[1,4096]{1,0:T(1,128)S(1)} fusion(f32[2048,1]{0,1:T(1,128)S(1)} %bitcast.809, f32[2048,4096]{1,0:T(8,128)} %param.99), kind=kOutput, calls=%fused_computation.530 | convolution fusion | flops 100663296 | bytes 33579008 | tf_op jit(solution)/shard_map/dot_general | solution.py:18
  80.7 38.6 %all-reduce.13 = (f32[8]{0:T(128)S(1)}, f32[4096]{0:T(1024)S(1)}, f32[8]{0:T(128)S(1)}, f32[]{:T(128)}, f32[8,8]{1,0:T(8,128)S(1)}) all-reduce(f32[8]{0:T(128)S(1)} %convolution_bitcast_fusion.45, f32[4096]{0:T(1024)S(1)} %bitcast.818, f32[8]{0:T(128)S(1)} %convolution_bitcast_fusion.46, ...), channel_id=1, replica_groups=mesh['prow'=8,'pcol'=4] {'prow'}, use_global_device_ids=true, to_apply=%region_5.6 | all-reduce | flops 4177 | bytes 33416 | tf_op jit(solution)/shard_map/psum | solution.py:67
  121.5 2.9 all-reduce.27.cloned.1.call-done
  124.3 1.6 fusion.317
  127.5 30.7 %fusion.322 = f32[1,2048]{1,0:T(1,128)S(1)} fusion(f32[4096,1]{0,1:T(1,128)S(1)} %bitcast.802, f32[2048,4096]{1,0:T(8,128)} %param.99), kind=kOutput, calls=%fused_computation.531 | convolution fusion | flops 100663296 | bytes 33579008 | tf_op jit(solution)/shard_map/dot_general | solution.py:18
  158.6 11.4 %all-reduce.21 = (f32[9]{0:T(128)S(1)}, f32[]{:T(128)}, f32[8,9]{1,0:T(8,128)S(1)}, f32[8]{0:T(128)S(1)}, f32[2048]{0:T(1024)S(1)}, /*index=5*/f32[8]{0:T(128)S(1)}) all-reduce(f32[9]{0:T(128)S(1)} %convolution_bitcast_fusion.44, f32[]{:T(128)} %get-tuple-element.757, ...), channel_id=1, replica_groups=mesh['prow'=8,'pcol'=4] {'pcol'}, use_global_device_ids=true, to_apply=%region_9.10 | all-reduce | flops 2146 | bytes 17168 | tf_op jit(solution)/shard_map/psum | solution.py:96
  173.6 0.9 fusion.228
  177.3 19.5 %fusion.323 = f32[1,4096]{1,0:T(1,128)S(1)} fusion(f32[2048,1]{0,1:T(1,128)S(1)} %bitcast.805, f32[2048,4096]{1,0:T(8,128)} %param.99), kind=kOutput, calls=%fused_computation.532 | convolution fusion | flops 100663296 | bytes 33579008 | tf_op jit(solution)/shard_map/dot_general | solution.py:18
  197.5 36.5 %all-reduce.12 = (f32[8]{0:T(128)S(1)}, f32[4096]{0:T(1024)S(1)}, f32[8]{0:T(128)S(1)}, f32[8]{0:T(128)S(1)}, f32[]{:T(128)}, /*index=5*/f32[8,8]{1,0:T(8,128)S(1)}) all-reduce(f32[8]{0:T(128)S(1)} %convolution_bitcast_fusion.40, f32[4096]{0:T(1024)S(1)} %bitcast.813, ...), channel_id=1, replica_groups=mesh['prow'=8,'pcol'=4] {'prow'}, use_global_device_ids=true, to_apply=%region_20.21 | all-reduce | flops 4185 | bytes 33480 | tf_op jit(solution)/shard_map/psum | solution.py:67
  240.9 30.7 %fusion.324 = f32[1,2048]{1,0:T(1,128)S(1)} fusion(f32[4096,1]{0,1:T(1,128)S(1)} %bitcast.774, f32[2048,4096]{1,0:T(8,128)} %param.99), kind=kOutput, calls=%fused_computation.533 | convolution fusion | flops 100663296 | bytes 33579008 | tf_op jit(solution)/shard_map/dot_general | solution.py:18
  272.0 11.2 %all-reduce.20 = (f32[9]{0:T(128)S(1)}, f32[]{:T(128)}, f32[8,9]{1,0:T(8,128)S(1)}, f32[8]{0:T(128)S(1)}, f32[2048]{0:T(1024)S(1)}, /*index=5*/f32[8]{0:T(128)S(1)}) all-reduce(f32[9]{0:T(128)S(1)} %convolution_bitcast_fusion.39, f32[]{:T(128)} %get-tuple-element.750, ...), channel_id=1, replica_groups=mesh['prow'=8,'pcol'=4] {'pcol'}, use_global_device_ids=true, to_apply=%region_23.24 | all-reduce | flops 2146 | bytes 17168 | tf_op jit(solution)/shard_map/psum | solution.py:96
  287.5 4.7 scatter.170
  292.2 0.9 fusion.223
  293.1 0.9 fusion.279
  296.4 19.5 %fusion.325 = f32[1,4096]{1,0:T(1,128)S(1)} fusion(f32[2048,1]{0,1:T(1,128)S(1)} %bitcast.777, f32[2048,4096]{1,0:T(8,128)} %param.99), kind=kOutput, calls=%fused_computation.534 | convolution fusion | flops 100663296 | bytes 33579008 | tf_op jit(solution)/shard_map/dot_general | solution.py:18
  316.6 34.1 %all-reduce.11 = (f32[8]{0:T(128)S(1)}, f32[4096]{0:T(1024)S(1)}, f32[8]{0:T(128)S(1)}, f32[8]{0:T(128)S(1)}, f32[]{:T(128)}, /*index=5*/f32[8,8]{1,0:T(8,128)S(1)}) all-reduce(f32[8]{0:T(128)S(1)} %convolution_bitcast_fusion.35, f32[4096]{0:T(1024)S(1)} %bitcast.811, ...), channel_id=1, replica_groups=mesh['prow'=8,'pcol'=4] {'prow'}, use_global_device_ids=true, to_apply=%region_34.35 | all-reduce | flops 4185 | bytes 33480 | tf_op jit(solution)/shard_map/psum | solution.py:67
  358.3 30.7 %fusion.326 = f32[1,2048]{1,0:T(1,128)S(1)} fusion(f32[4096,1]{0,1:T(1,128)S(1)} %bitcast.754, f32[2048,4096]{1,0:T(8,128)} %param.99), kind=kOutput, calls=%fused_computation.535 | convolution fusion | flops 100663296 | bytes 33579008 | tf_op jit(solution)/shard_map/dot_general | solution.py:18
  389.3 11.2 %all-reduce.19 = (f32[9]{0:T(128)S(1)}, f32[]{:T(128)}, f32[8,9]{1,0:T(8,128)S(1)}, f32[8]{0:T(128)S(1)}, f32[2048]{0:T(1024)S(1)}, /*index=5*/f32[8]{0:T(128)S(1)}) all-reduce(f32[9]{0:T(128)S(1)} %convolution_bitcast_fusion.34, f32[]{:T(128)} %get-tuple-element.743, ...), channel_id=1, replica_groups=mesh['prow'=8,'pcol'=4] {'pcol'}, use_global_device_ids=true, to_apply=%region_37.38 | all-reduce | flops 2146 | bytes 17168 | tf_op jit(solution)/shard_map/psum | solution.py:96
  404.4 4.7 scatter.180
  409.3 0.9 fusion.214
  410.3 0.9 fusion.272
  413.6 19.5 %fusion.327 = f32[1,4096]{1,0:T(1,128)S(1)} fusion(f32[2048,1]{0,1:T(1,128)S(1)} %bitcast.785, f32[2048,4096]{1,0:T(8,128)} %param.99), kind=kOutput, calls=%fused_computation.536 | convolution fusion | flops 100663296 | bytes 33579008 | tf_op jit(solution)/shard_map/dot_general | solution.py:18
  433.8 34.1 %all-reduce.10 = (f32[8]{0:T(128)S(1)}, f32[4096]{0:T(1024)S(1)}, f32[8]{0:T(128)S(1)}, f32[8]{0:T(128)S(1)}, f32[]{:T(128)}, /*index=5*/f32[8,8]{1,0:T(8,128)S(1)}) all-reduce(f32[8]{0:T(128)S(1)} %convolution_bitcast_fusion.30, f32[4096]{0:T(1024)S(1)} %bitcast.814, ...), channel_id=1, replica_groups=mesh['prow'=8,'pcol'=4] {'prow'}, use_global_device_ids=true, to_apply=%region_48.49 | all-reduce | flops 4185 | bytes 33480 | tf_op jit(solution)/shard_map/psum | solution.py:67
  475.6 30.7 %fusion.328 = f32[1,2048]{1,0:T(1,128)S(1)} fusion(f32[4096,1]{0,1:T(1,128)S(1)} %bitcast.758, f32[2048,4096]{1,0:T(8,128)} %param.99), kind=kOutput, calls=%fused_computation.537 | convolution fusion | flops 100663296 | bytes 33579008 | tf_op jit(solution)/shard_map/dot_general | solution.py:18
  506.6 11.2 %all-reduce.18 = (f32[9]{0:T(128)S(1)}, f32[]{:T(128)}, f32[8,9]{1,0:T(8,128)S(1)}, f32[8]{0:T(128)S(1)}, f32[2048]{0:T(1024)S(1)}, /*index=5*/f32[8]{0:T(128)S(1)}) all-reduce(f32[9]{0:T(128)S(1)} %convolution_bitcast_fusion.29, f32[]{:T(128)} %get-tuple-element.736, ...), channel_id=1, replica_groups=mesh['prow'=8,'pcol'=4] {'pcol'}, use_global_device_ids=true, to_apply=%region_51.52 | all-reduce | flops 2146 | bytes 17168 | tf_op jit(solution)/shard_map/psum | solution.py:96
  521.6 4.7 scatter.190
  526.6 0.9 fusion.204
  527.5 0.9 fusion.264
  530.8 19.5 %fusion.329 = f32[1,4096]{1,0:T(1,128)S(1)} fusion(f32[2048,1]{0,1:T(1,128)S(1)} %bitcast.789, f32[2048,4096]{1,0:T(8,128)} %param.99), kind=kOutput, calls=%fused_computation.538 | convolution fusion | flops 100663296 | bytes 33579008 | tf_op jit(solution)/shard_map/dot_general | solution.py:18
  550.9 34.1 %all-reduce.9 = (f32[8]{0:T(128)S(1)}, f32[4096]{0:T(1024)S(1)}, f32[8]{0:T(128)S(1)}, f32[8]{0:T(128)S(1)}, f32[]{:T(128)}, /*index=5*/f32[8,8]{1,0:T(8,128)S(1)}) all-reduce(f32[8]{0:T(128)S(1)} %convolution_bitcast_fusion.25, f32[4096]{0:T(1024)S(1)} %bitcast.815, ...), channel_id=1, replica_groups=mesh['prow'=8,'pcol'=4] {'prow'}, use_global_device_ids=true, to_apply=%region_62.63 | all-reduce | flops 4185 | bytes 33480 | tf_op jit(solution)/shard_map/psum | solution.py:67
  592.4 30.7 %fusion.330 = f32[1,2048]{1,0:T(1,128)S(1)} fusion(f32[4096,1]{0,1:T(1,128)S(1)} %bitcast.762, f32[2048,4096]{1,0:T(8,128)} %param.99), kind=kOutput, calls=%fused_computation.539 | convolution fusion | flops 100663296 | bytes 33579008 | tf_op jit(solution)/shard_map/dot_general | solution.py:18
  623.4 11.2 %all-reduce.17 = (f32[9]{0:T(128)S(1)}, f32[]{:T(128)}, f32[8,9]{1,0:T(8,128)S(1)}, f32[8]{0:T(128)S(1)}, f32[2048]{0:T(1024)S(1)}, /*index=5*/f32[8]{0:T(128)S(1)}) all-reduce(f32[9]{0:T(128)S(1)} %convolution_bitcast_fusion.24, f32[]{:T(128)} %get-tuple-element.729, ...), channel_id=1, replica_groups=mesh['prow'=8,'pcol'=4] {'pcol'}, use_global_device_ids=true, to_apply=%region_65.66 | all-reduce | flops 2146 | bytes 17168 | tf_op jit(solution)/shard_map/psum | solution.py:96
  638.7 4.7 scatter.200
  643.6 0.9 fusion.194
  644.5 0.9 fusion.256
  647.9 19.5 %fusion.331 = f32[1,4096]{1,0:T(1,128)S(1)} fusion(f32[2048,1]{0,1:T(1,128)S(1)} %bitcast.793, f32[2048,4096]{1,0:T(8,128)} %param.99), kind=kOutput, calls=%fused_computation.540 | convolution fusion | flops 100663296 | bytes 33579008 | tf_op jit(solution)/shard_map/dot_general | solution.py:18
  668.1 34.1 %all-reduce.8 = (f32[8]{0:T(128)S(1)}, f32[4096]{0:T(1024)S(1)}, f32[8]{0:T(128)S(1)}, f32[8]{0:T(128)S(1)}, f32[]{:T(128)}, /*index=5*/f32[8,8]{1,0:T(8,128)S(1)}) all-reduce(f32[8]{0:T(128)S(1)} %convolution_bitcast_fusion.20, f32[4096]{0:T(1024)S(1)} %bitcast.816, ...), channel_id=1, replica_groups=mesh['prow'=8,'pcol'=4] {'prow'}, use_global_device_ids=true, to_apply=%region_76.77 | all-reduce | flops 4185 | bytes 33480 | tf_op jit(solution)/shard_map/psum | solution.py:67
  710.1 30.7 %fusion.332 = f32[1,2048]{1,0:T(1,128)S(1)} fusion(f32[4096,1]{0,1:T(1,128)S(1)} %bitcast.766, f32[2048,4096]{1,0:T(8,128)} %param.99), kind=kOutput, calls=%fused_computation.541 | convolution fusion | flops 100663296 | bytes 33579008 | tf_op jit(solution)/shard_map/dot_general | solution.py:18
  741.1 11.2 %all-reduce.16 = (f32[9]{0:T(128)S(1)}, f32[]{:T(128)}, f32[8,9]{1,0:T(8,128)S(1)}, f32[8]{0:T(128)S(1)}, f32[2048]{0:T(1024)S(1)}, /*index=5*/f32[8]{0:T(128)S(1)}) all-reduce(f32[9]{0:T(128)S(1)} %convolution_bitcast_fusion.19, f32[]{:T(128)} %get-tuple-element.722, ...), channel_id=1, replica_groups=mesh['prow'=8,'pcol'=4] {'pcol'}, use_global_device_ids=true, to_apply=%region_79.80 | all-reduce | flops 2146 | bytes 17168 | tf_op jit(solution)/shard_map/psum | solution.py:96
  756.2 4.7 scatter.210
  761.2 0.9 fusion.184
  762.1 0.9 fusion.248
  765.4 19.5 %fusion.333 = f32[1,4096]{1,0:T(1,128)S(1)} fusion(f32[2048,1]{0,1:T(1,128)S(1)} %bitcast.797, f32[2048,4096]{1,0:T(8,128)} %param.99), kind=kOutput, calls=%fused_computation.542 | convolution fusion | flops 100663296 | bytes 33579008 | tf_op jit(solution)/shard_map/dot_general | solution.py:18
  785.5 34.1 %all-reduce.7 = (f32[8]{0:T(128)S(1)}, f32[4096]{0:T(1024)S(1)}, f32[8]{0:T(128)S(1)}, f32[8]{0:T(128)S(1)}, f32[]{:T(128)}, /*index=5*/f32[8,8]{1,0:T(8,128)S(1)}) all-reduce(f32[8]{0:T(128)S(1)} %convolution_bitcast_fusion.15, f32[4096]{0:T(1024)S(1)} %bitcast.817, ...), channel_id=1, replica_groups=mesh['prow'=8,'pcol'=4] {'prow'}, use_global_device_ids=true, to_apply=%region_90.91 | all-reduce | flops 4185 | bytes 33480 | tf_op jit(solution)/shard_map/psum | solution.py:67
  827.1 30.7 %fusion.334 = f32[1,2048]{1,0:T(1,128)S(1)} fusion(f32[4096,1]{0,1:T(1,128)S(1)} %bitcast.750, f32[2048,4096]{1,0:T(8,128)} %param.99), kind=kOutput, calls=%fused_computation.543 | convolution fusion | flops 100663296 | bytes 33579008 | tf_op jit(solution)/shard_map/dot_general | solution.py:18
  858.1 11.2 %all-reduce.15 = (f32[9]{0:T(128)S(1)}, f32[]{:T(128)}, f32[8,9]{1,0:T(8,128)S(1)}, f32[8]{0:T(128)S(1)}, f32[2048]{0:T(1024)S(1)}, /*index=5*/f32[8]{0:T(128)S(1)}) all-reduce(f32[9]{0:T(128)S(1)} %convolution_bitcast_fusion.14, f32[]{:T(128)} %get-tuple-element.715, ...), channel_id=1, replica_groups=mesh['prow'=8,'pcol'=4] {'pcol'}, use_global_device_ids=true, to_apply=%region_93.94 | all-reduce | flops 2146 | bytes 17168 | tf_op jit(solution)/shard_map/psum | solution.py:96
  872.9 4.7 scatter.220
  877.9 0.9 fusion.174
  878.8 0.9 fusion.240
  882.1 19.5 %fusion.335 = f32[1,4096]{1,0:T(1,128)S(1)} fusion(f32[2048,1]{0,1:T(1,128)S(1)} %bitcast.781, f32[2048,4096]{1,0:T(8,128)} %param.99), kind=kOutput, calls=%fused_computation.544 | convolution fusion | flops 100663296 | bytes 33579008 | tf_op jit(solution)/shard_map/dot_general | solution.py:18
  902.3 34.0 %all-reduce.6 = (f32[8]{0:T(128)S(1)}, f32[4096]{0:T(1024)S(1)}, f32[8]{0:T(128)S(1)}, f32[8]{0:T(128)S(1)}, f32[]{:T(128)}, /*index=5*/f32[8,8]{1,0:T(8,128)S(1)}) all-reduce(f32[8]{0:T(128)S(1)} %convolution_bitcast_fusion.10, f32[4096]{0:T(1024)S(1)} %bitcast.812, ...), channel_id=1, replica_groups=mesh['prow'=8,'pcol'=4] {'prow'}, use_global_device_ids=true, to_apply=%region_105.106 | all-reduce | flops 4185 | bytes 33480 | tf_op jit(solution)/shard_map/psum | solution.py:67
  943.6 30.7 %fusion.336 = f32[1,2048]{1,0:T(1,128)S(1)} fusion(f32[4096,1]{0,1:T(1,128)S(1)} %bitcast.770, f32[2048,4096]{1,0:T(8,128)} %param.99), kind=kOutput, calls=%fused_computation.545 | convolution fusion | flops 100663296 | bytes 33579008 | tf_op jit(solution)/shard_map/dot_general | solution.py:18
  974.6 11.1 %all-reduce.14 = (f32[9]{0:T(128)S(1)}, f32[]{:T(128)}, f32[8,9]{1,0:T(8,128)S(1)}, f32[8]{0:T(128)S(1)}, f32[2048]{0:T(1024)S(1)}, /*index=5*/f32[8]{0:T(128)S(1)}) all-reduce(f32[9]{0:T(128)S(1)} %convolution_bitcast_fusion.9, f32[]{:T(128)} %get-tuple-element.708, ...), channel_id=1, replica_groups=mesh['prow'=8,'pcol'=4] {'pcol'}, use_global_device_ids=true, to_apply=%region_106.107 | all-reduce | flops 2146 | bytes 17168 | tf_op jit(solution)/shard_map/psum | solution.py:96
  989.3 4.7 scatter.230
  994.3 0.9 fusion.232
  995.6 0.9 fusion.164
  997.8 32.9 %convolution_subtract_fusion = f32[2048,4096]{1,0:T(8,128)} fusion(f32[2048,4096]{1,0:T(8,128)} %param.99, f32[8,4096]{1,0:T(8,128)S(1)} %scatter.239, f32[8,4096]{1,0:T(8,128)S(1)} %scatter.235, f32[8,2048]{1,0:T(8,128)S(1)} %scatter.236, f32[8,2048]{1,0:T(8,128)S(1)} %copy.27), kind=kOutput, calls=%fused_computation | convolution fusion | flops 1619099648 | bytes 67502080 | tf_op jit(solution)/shard_map/dot_general | solution.py:137
  1030.6 2.3 select_select_fusion
  1032.9 5.8 scatter.240
  1039.7 1.8 fusion.2
  (293 shorter events, 77.7 us)
Async XLA Ops:
  7.2 42.8 %all-reduce.25.cloned.1.call-start = ((), (), s32[]{:S(2)}) async-start(), calls=%async_computation | async-start | bytes 2097152 | tf_op jit(solution)/shard_map/psum | solution.py:14
  9.5 114.8 %all-reduce.27.cloned.1.call-start = ((), (), s32[]{:S(2)}) async-start(), calls=%async_computation.1 | async-start | bytes 262144 | tf_op jit(solution)/shard_map/psum | solution.py:14
  882.1 114.7 %copy-start.1 = (f32[2048]{0:T(1024)S(1)}, f32[2048]{0:T(1024)}, u32[]{:S(2)}) copy-start(f32[2048]{0:T(1024)} %get-tuple-element.590) | copy-start | bytes 24580
  997.7 32.9 %copy-start.2 = (pred[2048]{0:T(1024)(128)(4,1)S(1)}, pred[2048]{0:T(1024)(128)(4,1)}, u32[]{:S(2)}) copy-start(pred[2048]{0:T(1024)(128)(4,1)} %fusion.145) | copy-start | bytes 6148
  997.8 41.9 %copy-start = (pred[9,4096]{1,0:T(8,128)(4,1)S(1)}, pred[9,4096]{1,0:T(8,128)(4,1)}, u32[]{:S(2)}) copy-start(pred[9,4096]{1,0:T(8,128)(4,1)} %iota_compare_fusion) | copy-start | bytes 110596
  997.8 41.9 %copy-start.3 = (pred[4096]{0:T(1024)(128)(4,1)S(1)}, pred[4096]{0:T(1024)(128)(4,1)}, u32[]{:S(2)}) copy-start(pred[4096]{0:T(1024)(128)(4,1)} %fusion.94) | copy-start | bytes 12292
  997.8 41.9 %copy-start.4 = (s32[8]{0:T(128)S(1)}, s32[8]{0:T(128)}, u32[]{:S(2)}) copy-start(s32[8]{0:T(128)} %iota_add_fusion.2) | copy-start | bytes 100
Sparse Core Ops, SparseCore 0:
  10.9 38.9 all-reduce.24
  53.3 71.0 all-reduce.26
where the time goes:
time: 1060 us; the launch traced here: 1050 us
  matrix products  483 us (46%)
  blocking collectives  369 us (35%)
  local copies, waits for them, and re-layouts  80.7 us (8%)
  between operations  56.4 us (5%)
  waiting for transfers between devices  38 us (4%)
  other arithmetic  21.1 us (2%)
    dot_general x134, matrix products, precise_dot(): return jnp.dot(left, right, precision=lax.Precision.HIGHEST)  447 us
    psum x8, blocking collectives, per_device(): lax.psum((precise_dot(masked, held_tile), precise_dot(v_rows, masked), pr...  280 us
    psum x8, blocking collectives, per_device(): lax.psum((precise_dot(held_tile, row_masked), precise_dot(y_cols, row_mas...  89.6 us
    psum x2, waiting for transfers between devices, from_root(): return lax.psum(jnp.where(mine, x, jnp.zeros_like(x)), axis)  38 us
    scatter x9, local copies, waits for them, and re-layouts, per_device(): v_rows = v_rows.at[i].set(v_new)  33.3 us
    dot_general x1, matrix products, per_device(): lax.dot_general(stack_left, stack_right, (((0,), (0,)), ((), ())), precis...  32.9 us
  transfers between devices with their start and end apart: 2, of which 2 were waited for; matrix products, arithmetic and copies ran while one was open for 4% of the time, Pallas kernels for 0%

commit v1 on v0

v1 whole, which is shorter than its diff:
```python
import functools

import jax
import jax.numpy as jnp
from jax import lax
from jax.experimental import pallas as pl
from jax.experimental.pallas import tpu as pltpu
from jax.sharding import PartitionSpec as P

NB = 8
EPS = 1e-06
LANES = 128
YC = 4
XC = 2
MESH = pl.DeviceIdType.MESH


def householder(alpha, sumsq):
    beta = jnp.where(alpha >= 0.0, -1.0, 1.0) * jnp.sqrt(sumsq + EPS)
    return beta, (beta - alpha) / beta, alpha - beta


def lane_sum(x):
    return jnp.sum(x, axis=1, keepdims=True)


def total(x):
    return jnp.sum(lane_sum(x), axis=0, keepdims=True)


def panel_kernel(np_, nq, a_hbm, left_o, right_o, scal_o,
                 a, strip, arows, colp, rowp, v_s, x_s, y_s, u_s, vb, ub,
                 ybuf, xbuf, column_s,
                 a_sem, strip_sem, arow_sem, col_ssem, col_rsem, row_ssem, row_rsem,
                 y_ssem, y_rsem, x_ssem, x_rsem):
    me_p = lax.axis_index("prow")
    me_q = lax.axis_index("pcol")
    rows, cols = a.shape
    rs, cs = rows // LANES, cols // LANES
    chunk = cols // YC
    per = chunk // LANES
    xper = rs // XC

    strip_cp = pltpu.make_async_copy(a_hbm.at[:, pl.ds(0, LANES)], strip, strip_sem)
    strip_cp.start()
    arow_cp = pltpu.make_async_copy(a_hbm.at[pl.ds(0, NB), :], arows, arow_sem)
    arow_cp.start()
    a_cps = []
    for c in range(YC):
        cp = pltpu.make_async_copy(
            a_hbm.at[:, pl.ds(c * chunk, chunk)], a.at[:, pl.ds(c * chunk, chunk)], a_sem.at[c])
        cp.start()
        a_cps.append(cp)

    barrier = pltpu.get_barrier_semaphore()
    for d in range(1, np_):
        pl.semaphore_signal(barrier, inc=1, device_id={"prow": lax.rem(me_p + d, np_)}, device_id_type=MESH)
    for d in range(1, nq):
        pl.semaphore_signal(barrier, inc=1, device_id={"pcol": lax.rem(me_q + d, nq)}, device_id_type=MESH)
    pl.semaphore_wait(barrier, np_ + nq - 2)

    lane8 = lax.broadcasted_iota(jnp.int32, (8, LANES), 1)
    sub8 = lax.broadcasted_iota(jnp.int32, (8, LANES), 0)
    row_gl = (me_p * rows + lax.broadcasted_iota(jnp.int32, (rs, LANES), 0) * LANES
              + lax.broadcasted_iota(jnp.int32, (rs, LANES), 1))
    col_gl = (me_q * cols + lax.broadcasted_iota(jnp.int32, (cs, LANES), 0) * LANES
              + lax.broadcasted_iota(jnp.int32, (cs, LANES), 1))

    strip_cp.wait()
    arow_cp.wait()

    def col_copy(d):
        return pltpu.make_async_remote_copy(
            src_ref=colp, dst_ref=colp, send_sem=col_ssem.at[d], recv_sem=col_rsem,
            device_id={"pcol": lax.rem(me_q + d, nq)}, device_id_type=MESH)

    def row_copy(i, d):
        return pltpu.make_async_remote_copy(
            src_ref=rowp.at[i], dst_ref=rowp.at[i], send_sem=row_ssem.at[i, d], recv_sem=row_rsem.at[i],
            device_id={"prow": lax.rem(me_p + d, np_)}, device_id_type=MESH)

    @pl.when(me_q == 0)
    def _():
        @pl.loop(0, rs)
        def _(s):
            t = strip[pl.ds(s * LANES, LANES), :].T
            for c in range(NB + 1):
                colp[c, pl.ds(s, 1), :] = t[c:c + 1, :]
        for d in range(1, nq):
            col_copy(d).start()

    @pl.when(me_p == 0)
    def _():
        for s in range(cs):
            blk = arows[:, s * LANES:(s + 1) * LANES]
            for i in range(NB):
                rowp[i, s:s + 1, :] = blk[i:i + 1, :]
        for i in range(2):
            for d in range(1, np_):
                row_copy(i, d).start()

    for ref in (v_s, x_s, y_s, u_s):
        ref[...] = jnp.zeros(ref.shape, jnp.float32)

    @pl.when(me_q != 0)
    def _():
        col_copy(1).wait_recv()

    column_s[...] = colp[0]

    def y_copy(i, d, c):
        lo, n = (0, 8 + per) if c == 0 else (8 + c * per, per)
        ref = ybuf.at[i, me_p, pl.ds(lo, n), :]
        return pltpu.make_async_remote_copy(
            src_ref=ref, dst_ref=ref, send_sem=y_ssem.at[d, c], recv_sem=y_rsem.at[lax.rem(i, 2), d, c],
            device_id={"prow": lax.rem(me_p + d, np_)}, device_id_type=MESH)

    def x_copy(i, d, c):
        lo, n = (0, 8 + xper) if c == 0 else (8 + c * xper, xper)
        ref = xbuf.at[i, me_q, pl.ds(lo, n), :]
        return pltpu.make_async_remote_copy(
            src_ref=ref, dst_ref=ref, send_sem=x_ssem.at[d, c], recv_sem=x_rsem.at[lax.rem(i, 2), d, c],
            device_id={"pcol": lax.rem(me_q + d, nq)}, device_id_type=MESH)

    def scalar_tile(first, second, vec, unit):
        tile = jnp.zeros((8, LANES), jnp.float32)
        for k, (ref, w) in enumerate(((first, vec), (second, vec), (first, unit), (second, unit))):
            s = lane_sum(jnp.sum(ref[...] * w[None], axis=1))
            tile = jnp.where(lane8 == k, s, tile)
        s = jnp.where(sub8[:, :1] == 0, total(vec * unit), total(vec * vec))
        return jnp.where(lane8 == 4, s, tile)

    def unpack(tile):
        return [jnp.broadcast_to(lane_sum(jnp.where(lane8 == k, tile, 0.0)), (8, LANES)) for k in range(5)]

    def combine(coef_a, ref_a, coef_b, ref_b):
        acc = coef_a[0:1] * ref_a[0] + coef_b[0:1] * ref_b[0]
        for j in range(1, NB):
            acc = acc + (coef_a[j:j + 1] * ref_a[j] + coef_b[j:j + 1] * ref_b[j])
        return acc

    @pl.loop(0, NB)
    def _(i):
        masked = jnp.where(row_gl >= i, column_s[...], 0.0)
        unit_r = (row_gl == i).astype(jnp.float32)
        column_s[...] = masked

        @pl.loop(0, rs)
        def _(s):
            row = jnp.broadcast_to(column_s[pl.ds(s, 1), :], (8, LANES))
            for g in range(LANES // 8):
                col = lane_sum(jnp.where(lane8 == sub8 + 8 * g, row, 0.0))
                vb[pl.ds(s * LANES + 8 * g, 8), :] = jnp.broadcast_to(col, (8, LANES))

        ybuf[i, me_p, 0:8, :] = scalar_tile(v_s, x_s, masked, unit_r)
        for c in range(YC):
            @pl.when(i == 0)
            def _(c=c):
                a_cps[c].wait()

            def body(g, accs):
                accs = list(accs)
                for k in range(8):
                    r = pl.ds(pl.multiple_of(g * 64 + 8 * k, 8), 8)
                    v = vb[r, :]
                    for j in range(per):
                        lo = c * chunk + j * LANES
                        m = (k % 2) * per + j
                        accs[m] = accs[m] + v * a[r, lo:lo + LANES]
                return tuple(accs)

            accs = lax.fori_loop(0, rows // 64, body, (jnp.zeros((8, LANES), jnp.float32),) * (2 * per))
            for j in range(per):
                t = 8 + c * per + j
                ybuf[i, me_p, t:t + 1, :] = jnp.sum(accs[j] + accs[per + j], axis=0, keepdims=True)
            for d in range(1, np_):
                y_copy(i, d, c).start()

        @pl.when(jnp.logical_and(me_p == 0, i < NB - 2))
        def _():
            for d in range(1, np_):
                row_copy(i + 2, d).start()

        @pl.when(me_p != 0)
        def _():
            row_copy(i, 1).wait_recv()

        for c in range(YC):
            for d in range(1, np_):
                y_copy(i, d, c).wait()
        summed = ybuf[i, 0]
        for p in range(1, np_):
            summed = summed + ybuf[i, p]
        v_coef, x_coef, v_at, x_at, misc = unpack(summed[0:8])
        beta, tau, denom = householder(misc[0:1], misc[1:2])
        row_eff = rowp[i] - combine(v_at, y_s, x_at, u_s)
        inv = 1.0 / denom
        trans = (summed[8:] - combine(v_coef, y_s, x_coef, u_s) - beta * row_eff) * inv
        y_new = jnp.where(col_gl > i, tau * trans, 0.0)
        v_s[i] = (masked - beta * unit_r) * inv
        y_s[i] = y_new
        scal_o[0, pl.ds(i, 1), :] = beta
        scal_o[2, pl.ds(i, 1), :] = tau

        row_m = jnp.where(col_gl > i, row_eff - y_new, 0.0)
        unit_c = (col_gl == i + 1).astype(jnp.float32)
        ub[...] = row_m
        xbuf[i, me_q, 0:8, :] = scalar_tile(y_s, u_s, row_m, unit_c)
        for c in range(XC):
            @pl.loop(c * xper, (c + 1) * xper)
            def _(s):
                us = [jnp.broadcast_to(ub[j:j + 1, :], (8, LANES)) for j in range(cs)]
                tile = jnp.zeros((8, LANES), jnp.float32)
                for g in range(LANES // 8):
                    r = pl.ds(pl.multiple_of(s * LANES + 8 * g, 8), 8)
                    p0 = us[0] * a[r, 0:LANES]
                    p1 = us[1] * a[r, LANES:2 * LANES]
                    for j in range(2, cs, 2):
                        p0 = p0 + us[j] * a[r, j * LANES:(j + 1) * LANES]
                        p1 = p1 + us[j + 1] * a[r, (j + 1) * LANES:(j + 2) * LANES]
                    tile = jnp.where(lane8 == sub8 + 8 * g, lane_sum(p0 + p1), tile)
                xbuf[i, me_q, pl.ds(8 + s, 1), :] = jnp.sum(tile, axis=0, keepdims=True)
            for d in range(1, nq):
                x_copy(i, d, c).start()
        for c in range(XC):
            for d in range(1, nq):
                x_copy(i, d, c).wait()
        xsum = xbuf[i, 0]
        for q in range(1, nq):
            xsum = xsum + xbuf[i, q]
        y_coef, u_coef, y_at, u_at, misc2 = unpack(xsum[0:8])
        beta2, tau2, denom2 = householder(misc2[0:1], misc2[1:2])
        col_next = colp[i + 1] - combine(y_at, v_s, u_at, x_s)
        inv2 = 1.0 / denom2
        prod = (xsum[8:] - combine(y_coef, v_s, u_coef, x_s) - beta2 * col_next) * inv2
        x_new = jnp.where(row_gl > i, tau2 * prod, 0.0)
        x_s[i] = x_new
        u_s[i] = (row_m - beta2 * unit_c) * inv2
        scal_o[1, pl.ds(i, 1), :] = beta2
        scal_o[3, pl.ds(i, 1), :] = tau2
        column_s[...] = col_next - x_new

    for s in range(rs):
        left_o[0:NB, s * LANES:(s + 1) * LANES] = v_s[:, s, :]
        left_o[NB:, s * LANES:(s + 1) * LANES] = x_s[:, s, :]
    for s in range(cs):
        right_o[0:NB, s * LANES:(s + 1) * LANES] = y_s[:, s, :]
        right_o[NB:, s * LANES:(s + 1) * LANES] = u_s[:, s, :]

    @pl.when(me_q == 0)
    def _():
        for d in range(1, nq):
            col_copy(d).wait_send()

    @pl.when(me_p == 0)
    def _():
        @pl.loop(0, NB)
        def _(i):
            for d in range(1, np_):
                row_copy(i, d).wait_send()


def reduce_panel(matrix, np_, nq):
    rows, cols = matrix.shape
    rs, cs = rows // LANES, cols // LANES
    f32 = jnp.float32
    vmem = pl.BlockSpec(memory_space=pltpu.VMEM)
    dma = pltpu.SemaphoreType.DMA
    return pl.pallas_call(
        functools.partial(panel_kernel, np_, nq),
        out_shape=(jax.ShapeDtypeStruct((2 * NB, rows), f32),
                   jax.ShapeDtypeStruct((2 * NB, cols), f32),
                   jax.ShapeDtypeStruct((4, NB, LANES), f32)),
        in_specs=[pl.BlockSpec(memory_space=pl.ANY)],
        out_specs=(vmem, vmem, vmem),
        scratch_shapes=[
            pltpu.VMEM((rows, cols), f32),
            pltpu.VMEM((rows, LANES), f32),
            pltpu.VMEM((NB, cols), f32),
            pltpu.VMEM((NB + 1, rs, LANES), f32),
            pltpu.VMEM((NB, cs, LANES), f32),
            pltpu.VMEM((NB, rs, LANES), f32),
            pltpu.VMEM((NB, rs, LANES), f32),
            pltpu.VMEM((NB, cs, LANES), f32),
            pltpu.VMEM((NB, cs, LANES), f32),
            pltpu.VMEM((rows, LANES), f32),
            pltpu.VMEM((cs, LANES), f32),
            pltpu.VMEM((NB, np_, 8 + cs, LANES), f32),
            pltpu.VMEM((NB, nq, 8 + rs, LANES), f32),
            pltpu.VMEM((rs, LANES), f32),
            dma((YC,)), dma, dma,
            dma((nq,)), dma, dma((NB, np_)), dma((NB,)),
            dma((np_, YC)), dma((2, np_, YC)), dma((nq, XC)), dma((2, nq, XC)),
        ],
        compiler_params=pltpu.CompilerParams(
            collective_id=0, has_side_effects=True, vmem_limit_bytes=60 * 1024 * 1024),
    )(matrix)


def pieces(x):
    hi = x.astype(jnp.bfloat16)
    rest = x - hi.astype(jnp.float32)
    mid = rest.astype(jnp.bfloat16)
    lo = (rest - mid.astype(jnp.float32)).astype(jnp.bfloat16)
    return hi, mid, lo


def update_kernel(a_ref, left_ref, right_ref, scal_ref, out_ref):
    me_p = lax.axis_index("prow")
    me_q = lax.axis_index("pcol")
    step = pl.program_id(0)
    block, cols = a_ref.shape
    lh, lm, ll = pieces(left_ref[...])
    rh, rm, rl = pieces(right_ref[...])
    left = jnp.concatenate([lh, lh, lh, lm, lm, ll], axis=0)
    right = jnp.concatenate([rh, rm, rl, rh, rm, rh], axis=0)
    dims = (((0,), (0,)), ((), ()))
    out_ref[...] = a_ref[...] - lax.dot_general(left, right, dims, preferred_element_type=jnp.float32)

    k = left.shape[0]
    src = lax.broadcasted_iota(jnp.int32, (k, LANES), 0)
    lane = lax.broadcasted_iota(jnp.int32, (k, LANES), 1)
    pick = jnp.logical_and(
        lane < NB, (src == lane) | (src == lane + 6 * NB) | (src == lane + 10 * NB))
    vt = lax.dot_general(left, jnp.where(pick, 1.0, 0.0).astype(jnp.bfloat16), dims,
                         preferred_element_type=jnp.float32)

    @pl.when(me_q == 0)
    def _():
        lanes = lax.broadcasted_iota(jnp.int32, (block, LANES), 1)
        out_ref[:, 0:LANES] = jnp.where(lanes < NB, vt, out_ref[:, 0:LANES])

    @pl.when(jnp.logical_and(me_p == 0, step == 0))
    def _():
        out_ref[0:NB, :] = right_ref[NB:, :]

        @pl.when(me_q == 0)
        def _():
            r = lax.broadcasted_iota(jnp.int32, (NB, LANES), 0)
            c = lax.broadcasted_iota(jnp.int32, (NB, LANES), 1)
            out_ref[0:NB, 0:LANES] = jnp.where(
                c < r, vt[0:NB, :],
                jnp.where(c == r, scal_ref[0], jnp.where(c == r + 1, scal_ref[1], right_ref[NB:, 0:LANES])))


def apply_panel(matrix, left, right, scal):
    rows, cols = matrix.shape
    block = min(rows, 256)
    return pl.pallas_call(
        update_kernel,
        out_shape=jax.ShapeDtypeStruct((rows, cols), jnp.float32),
        grid=(rows // block,),
        in_specs=[
            pl.BlockSpec((block, cols), lambda i: (i, 0)),
            pl.BlockSpec((2 * NB, block), lambda i: (0, i)),
            pl.BlockSpec((2 * NB, cols), lambda i: (0, 0)),
            pl.BlockSpec((4, NB, LANES), lambda i: (0, 0, 0)),
        ],
        out_specs=pl.BlockSpec((block, cols), lambda i: (i, 0)),
        compiler_params=pltpu.CompilerParams(vmem_limit_bytes=48 * 1024 * 1024),
    )(matrix, left, right, scal)


def solution(mesh):
    np_, nq = mesh.shape["prow"], mesh.shape["pcol"]

    def per_device(matrix):
        left, right, scal = reduce_panel(matrix, np_, nq)
        return apply_panel(matrix, left, right, scal), scal[2:4, :, 0]

    return jax.shard_map(
        per_device, mesh=mesh, in_specs=(P("prow", "pcol"),),
        out_specs=(P("prow", "pcol"), P()), check_vma=False)
```

time: 1060 us -> 170 us (0.16); the launches traced: 1050 us -> 170 us
  matrix products: 483 us -> 0 us
  blocking collectives: 369 us -> 0 us
  Pallas kernels: 0 us -> 166 us
  local copies, waits for them, and re-layouts: 80.7 us -> 3.21 us
  between operations: 56.4 us -> 0.65 us
  waiting for transfers between devices: 38 us -> 0 us
  other arithmetic: 21.1 us -> 0 us
    dot_general x151 -> x0, matrix products: 483 us -> none  [the longest x134 447 us: precise_dot(): return jnp.dot(left, right, precision=lax.Precision.HIGHEST)]
    psum x16 -> x0, blocking collectives: 369 us -> none  [the longest x8 280 us: per_device(): lax.psum((precise_dot(masked, held_tile), precise_dot(v_rows, masked), pr...]
    pallas_call x0 -> x2, Pallas kernels: none -> 166 us  [the longest x1 142 us: reduce_panel(): pl.pallas_call(functools.partial(panel_kernel, np_, nq), out_shape=(jax.S...]
    scatter x49 -> x0, local copies, waits for them, and re-layouts: 50.5 us -> none  [the longest x9 33.3 us: per_device(): v_rows = v_rows.at[i].set(v_new)]
    psum x2 -> x0, waiting for transfers between devices: 38 us -> none  [from_root(): return lax.psum(jnp.where(mine, x, jnp.zeros_like(x)), axis)]
    slice x47 -> x1, local copies, waits for them, and re-layouts: 26.9 us -> 0.65 us  [per_device(): return (apply_panel(matrix, left, right, scal), scal[2:4, :, 0])]
  transfers between devices with their start and end apart: 2 -> 0, of which waited for: 2 -> 0; matrix products, arithmetic and copies ran while one was open for 4% -> 0% of each run, Pallas kernels for 0% -> 0%
where the time goes in v1:
time: 170 us
  Pallas kernels  166 us (98%)
  local copies, waits for them, and re-layouts  3.21 us (2%)
    pallas_call x1, Pallas kernels, reduce_panel(): pl.pallas_call(functools.partial(panel_kernel, np_, nq), out_shape=(jax.S...  142 us
    pallas_call x1, Pallas kernels, apply_panel(): pl.pallas_call(update_kernel, out_shape=jax.ShapeDtypeStruct((rows, cols)...  24.2 us

profile of v1, /device:TPU:0, one launch (start us, length us, event | category | flops | bytes accessed | tf_op | source)
XLA Modules:
  0.0 169.9 jit_solution(3094639716584757338)
XLA Ops:
  0.6 141.8 %shard_map.30 = (f32[16,2048]{1,0:T(8,128)}, f32[16,4096]{1,0:T(8,128)}, f32[4,8,128]{2,1,0:T(8,128)}) custom-call(f32[2048,4096]{1,0:T(8,128)} %a_ref.1), custom_call_target="tpu_custom_call" | custom-call | tf_op jit(solution)/shard_map/pallas_call | solution.py:269
  142.5 0.0 copy-start
  142.5 0.9 copy-done
  143.4 0.0 copy-start.1
  143.4 0.9 copy-done.1
  144.3 0.0 copy-start.2
  144.3 0.7 copy-done.2
  145.0 24.2 %shard_map.31 = f32[2048,4096]{1,0:T(8,128)} custom-call(f32[2048,4096]{1,0:T(8,128)} %a_ref.1, f32[16,2048]{1,0:T(8,128)S(1)} %copy-done.1, f32[16,4096]{1,0:T(8,128)S(1)} %copy-done, f32[4,8,128]{2,1,0:T(8,128)S(1)} %copy-done.2), custom_call_target="tpu_custom_call" | custom-call | tf_op jit(solution)/shard_map/pallas_call | solution.py:349
  169.3 0.6 slice_reduce_fusion
Async XLA Ops:
  142.5 1.0 copy-start
  143.4 0.9 copy-start.1
  144.3 0.7 copy-start.2

commit v2 on v1

--- a/solution.py
+++ b/solution.py
@@ -145,7 +145,7 @@
         unit_r = (row_gl == i).astype(jnp.float32)
         column_s[...] = masked
 
-        @pl.loop(0, rs)
+        @pl.loop(0, rs, unroll=min(8, rs))
         def _(s):
             row = jnp.broadcast_to(column_s[pl.ds(s, 1), :], (8, LANES))
             for g in range(LANES // 8):
@@ -207,7 +207,7 @@
         ub[...] = row_m
         xbuf[i, me_q, 0:8, :] = scalar_tile(y_s, u_s, row_m, unit_c)
         for c in range(XC):
-            @pl.loop(c * xper, (c + 1) * xper)
+            @pl.loop(c * xper, (c + 1) * xper, unroll=min(4, xper))
             def _(s):
                 us = [jnp.broadcast_to(ub[j:j + 1, :], (8, LANES)) for j in range(cs)]
                 tile = jnp.zeros((8, LANES), jnp.float32)

time: 170 us -> 152 us (0.89)
  Pallas kernels: 166 us -> 148 us
    pallas_call x1, Pallas kernels: 142 us -> 124 us  [reduce_panel(): pl.pallas_call(functools.partial(panel_kernel, np_, nq), out_shape=(jax.S...]
where the time goes in v2:
time: 152 us
  Pallas kernels  148 us (97%)
  local copies, waits for them, and re-layouts  3.21 us (2%)
    pallas_call x1, Pallas kernels, reduce_panel(): pl.pallas_call(functools.partial(panel_kernel, np_, nq), out_shape=(jax.S...  124 us
    pallas_call x1, Pallas kernels, apply_panel(): pl.pallas_call(update_kernel, out_shape=jax.ShapeDtypeStruct((rows, cols)...  24.2 us

profile of v2, /device:TPU:0, one launch (start us, length us, event | category | flops | bytes accessed | tf_op | source)
XLA Modules:
  0.0 152.0 jit_solution(9713773125473408838)
XLA Ops:
  0.6 124.0 %shard_map.30 = (f32[16,2048]{1,0:T(8,128)}, f32[16,4096]{1,0:T(8,128)}, f32[4,8,128]{2,1,0:T(8,128)}) custom-call(f32[2048,4096]{1,0:T(8,128)} %a_ref.1), custom_call_target="tpu_custom_call" | custom-call | tf_op jit(solution)/shard_map/pallas_call | solution.py:269
  124.6 0.0 copy-start
  124.6 0.9 copy-done
  125.6 0.0 copy-start.1
  125.6 0.9 copy-done.1
  126.5 0.0 copy-start.2
  126.5 0.7 copy-done.2
  127.2 24.2 %shard_map.31 = f32[2048,4096]{1,0:T(8,128)} custom-call(f32[2048,4096]{1,0:T(8,128)} %a_ref.1, f32[16,2048]{1,0:T(8,128)S(1)} %copy-done.1, f32[16,4096]{1,0:T(8,128)S(1)} %copy-done, f32[4,8,128]{2,1,0:T(8,128)S(1)} %copy-done.2), custom_call_target="tpu_custom_call" | custom-call | tf_op jit(solution)/shard_map/pallas_call | solution.py:349
  151.4 0.6 slice_reduce_fusion
Async XLA Ops:
  124.6 1.0 copy-start
  125.6 0.9 copy-start.1
  126.5 0.7 copy-start.2
